TPU v7x, 256 devices: a whole 4x4x8 slice. The times are simulated.
256 devices in a mesh: dp: 32 (over x, z_lo, core), head: 8 (over y, z_hi).
Axes of the slice: x: 4, y: 4, z: 8 (z_hi: 2, z_lo: 4; z = z_hi * 4 + z_lo), core: 2. Of those that a mesh axis runs over, the one named last changes fastest.
Arguments:
- frames_in: bfloat16 [32, 8, 320, 640], P('dp', 'head'), may hold values from -6 to 6
- ln1_gain: float32 [1280], replicated, may hold values from 0.25 to 1.75
- ln1_bias: float32 [1280], replicated, may hold values from -3 to 3
- qkv_weight: bfloat16 [1280, 3, 1024], P('dp', None, 'head'), may hold values from -0.1875 to 0.1875
- qv_bias: float32 [2, 1024], P(None, 'head'), may hold values from -3 to 3
- out_weight: bfloat16 [1024, 1280], P(('head', 'dp')), may hold values from -0.1875 to 0.1875
- out_bias: float32 [1280], P('head'), may hold values from -3 to 3
- ln2_gain: float32 [1280], replicated, may hold values from 0.25 to 1.75
- ln2_bias: float32 [1280], replicated, may hold values from -3 to 3
- fc1_weight: bfloat16 [1280, 5120], P('dp', 'head'), may hold values from -0.15625 to 0.15625
- fc1_bias: float32 [5120], P('head'), may hold values from -3 to 3
- fc2_weight: bfloat16 [5120, 1280], P(('head', 'dp')), may hold values from -0.078125 to 0.078125
- fc2_bias: float32 [1280], P('head'), may hold values from -3 to 3
- server_of_clip: int32 [32], replicated, may hold values from 0 to 7
Outputs:
- encoded: bfloat16 [32, 8, 320, 640], P('dp', 'head')
All inputs are finite; a program needn't handle non-finite values.
Results may differ from a plain program's by a relative error of at most 0.014.
Values may be sent and summed in bfloat16 or wider, within the bound.
No kernel may reach another device: no remote copies, remote signals or barrier semaphores. Data moves between devices by JAX's collectives and lax.ppermute only.
A program may use at most 64 MiB of HBM per device.

v0:
```python
import jax
import jax.numpy as jnp
from jax import lax
from jax.sharding import Mesh
from jax.sharding import PartitionSpec as P

HDIM = 64
HEAD = ("head_0", "head_1")
HEAD_DP = ("head_0", "head_1", "dp")
epsilon = 1e-05


def laid_out(blocks, dim):
    dims = list(blocks.shape[1:])
    dims[dim] *= blocks.shape[0]
    return jnp.moveaxis(blocks, 0, dim).reshape(dims)


def sent_to_all(value, axis):
    copies = jnp.broadcast_to(value, (lax.axis_size(axis), *value.shape))
    return lax.all_to_all(copies, axis, split_axis=0, concat_axis=0, tiled=True)


def gather_directly(value, axis, dim):
    return laid_out(sent_to_all(value, axis), dim)


def own_rows(terms, axes):
    total = terms.astype(jnp.bfloat16)
    for axis in axes:
        total = lax.psum_scatter(total, axis, scatter_dimension=0, tiled=True)
    return total.astype(jnp.float32)


def layer_norm(matrix, gain_row, shift_row):
    floats = matrix.astype(jnp.float32)
    center = jnp.mean(floats, axis=-1, keepdims=True)
    spread = jnp.mean(jnp.square(floats - center), axis=-1, keepdims=True)
    return ((floats - center) * lax.rsqrt(spread + epsilon) * gain_row + shift_row).astype(
        jnp.bfloat16
    )


def normalize(residual_in, gain_row, shift_row):
    whole_rows = lax.all_gather(residual_in, HEAD, axis=1, tiled=True)
    return layer_norm(whole_rows, gain_row, shift_row)


def attend(queries, key_rows, value_rows):

    def single(triple):
        query_head, key_head, value_head = triple
        scores = jnp.dot(query_head, key_head.T, preferred_element_type=jnp.float32)
        maxima = jnp.max(scores, axis=-1, keepdims=True)
        weights = jnp.exp(scores - maxima)
        probability = (weights / jnp.sum(weights, axis=-1, keepdims=True)).astype(jnp.bfloat16)
        return jnp.dot(probability, value_head, preferred_element_type=jnp.float32).astype(
            jnp.bfloat16
        )

    per_head = lax.map(
        single,
        (jnp.swapaxes(queries, 0, 1), jnp.swapaxes(key_rows, 0, 1), jnp.swapaxes(value_rows, 0, 1)),
    )
    return jnp.swapaxes(per_head, 0, 1).reshape(queries.shape[0], -1)


def slot_order(server_list):
    clip_count = server_list.shape[0]
    indices = jnp.arange(clip_count, dtype=jnp.int32)
    earlier = (server_list[None, :] < server_list[:, None]) | (
        server_list[None, :] == server_list[:, None]
    ) & (indices[None, :] < indices[:, None])
    slot_of = jnp.sum(earlier.astype(jnp.int32), axis=1)
    return jnp.sum(jnp.where(slot_of[None, :] == indices[:, None], indices[None, :], 0), axis=1)


def regroup(block_rows, clip_order):
    group_size = lax.axis_size("dp")
    piece_rows = block_rows.reshape(group_size, -1)
    shuffled = lax.all_to_all(piece_rows, "dp", split_axis=0, concat_axis=0, tiled=True)
    picked = jnp.take(shuffled, clip_order, axis=0)
    returned = lax.all_to_all(picked, "dp", split_axis=0, concat_axis=0, tiled=True)
    return returned.reshape(block_rows.shape)


def block_term(operand, weight_rows, row_count, frame_count, local_width):
    blocks = row_count // frame_count
    product = jnp.dot(operand, weight_rows, preferred_element_type=jnp.float32)
    return (
        product.reshape(frame_count, blocks, local_width)
        .transpose(1, 0, 2)
        .reshape(blocks * frame_count, local_width)
    )


def on_device(
    frames_in,
    ln1_gain,
    ln1_bias,
    qkv_weight,
    qv_bias,
    out_weight,
    out_bias,
    ln2_gain,
    ln2_bias,
    fc1_weight,
    fc1_bias,
    fc2_weight,
    fc2_bias,
    server_of_clip,
):
    clip_order = slot_order(server_of_clip)
    group_rows = frames_in.shape[2]
    local_width = frames_in.shape[3] // 4
    frame_count = group_rows * 4
    residual_in = frames_in[0, 0].reshape(frame_count, local_width)
    residual_in = regroup(residual_in, clip_order)
    head_count = lax.axis_size(HEAD)
    normed_one = normalize(residual_in, ln1_gain, ln1_bias)
    column_count = qkv_weight.shape[2]
    weight_piece = lax.all_gather(qkv_weight, "dp", axis=0, tiled=True)
    operand = normed_one
    projected = jnp.dot(
        operand, weight_piece.reshape(weight_piece.shape[0], -1), preferred_element_type=jnp.float32
    ).reshape(frame_count, 3, column_count)
    queries = (
        ((projected[:, 0] + qv_bias[0]) * HDIM ** (-0.5))
        .astype(jnp.bfloat16)
        .reshape(frame_count, -1, HDIM)
    )
    key_rows = projected[:, 1].astype(jnp.bfloat16).reshape(frame_count, -1, HDIM)
    value_rows = (projected[:, 2] + qv_bias[1]).astype(jnp.bfloat16).reshape(frame_count, -1, HDIM)
    context = attend(queries, key_rows, value_rows)
    output_rows = lax.all_gather(out_weight, "dp", axis=0, tiled=True)
    carried = residual_in.astype(jnp.float32) + out_bias
    whole_context = gather_directly(context, HEAD, 1)
    split_rows = output_rows.reshape(output_rows.shape[0], head_count, local_width)
    feature_columns = lax.all_to_all(
        split_rows, HEAD, split_axis=1, concat_axis=0, tiled=True
    ).reshape(-1, local_width)
    attended = (
        carried + jnp.dot(whole_context, feature_columns, preferred_element_type=jnp.float32)
    ).astype(jnp.bfloat16)
    normed_two = normalize(attended, ln2_gain, ln2_bias)
    operand = normed_two
    hidden_sums = jnp.dot(
        operand, gather_directly(fc1_weight, "dp", 0), preferred_element_type=jnp.float32
    )
    hidden = jax.nn.gelu(hidden_sums + fc1_bias, approximate=False).astype(jnp.bfloat16)
    down_rows = lax.all_gather(fc2_weight, "dp", axis=0, tiled=True)
    kept = attended.astype(jnp.float32) + fc2_bias
    layer_out = (
        kept
        + own_rows(
            block_term(
                hidden, down_rows, frame_count * lax.axis_size(HEAD), frame_count, local_width
            ),
            HEAD,
        )
    ).astype(jnp.bfloat16)
    return layer_out.reshape(1, 1, group_rows, 4 * local_width)


def solution(mesh):
    torus = Mesh(mesh.devices.reshape(mesh.shape["dp"], 4, 2), ("dp", "head_0", "head_1"))
    return jax.shard_map(
        on_device,
        mesh=torus,
        in_specs=(
            P("dp", HEAD, None, None),
            P(),
            P(),
            P("dp", None, HEAD),
            P(None, HEAD),
            P(HEAD_DP, None),
            P(HEAD),
            P(),
            P(),
            P("dp", HEAD),
            P(HEAD),
            P(HEAD_DP, None),
            P(HEAD),
            P(),
        ),
        out_specs=P("dp", HEAD, None, None),
        check_vma=False,
    )
```

profile of v0, /device:TPU:2, one launch (start us, length us, event | category | flops | bytes accessed | tf_op | source)
XLA Modules:
  0.0 519.4 jit_solution(1292017763583869009)
XLA Ops:
  7.4 2.4 all_to_all.38
  10.3 3.1 reduce.9
  14.3 9.1 %all-to-all-start = ((bf16[32,2,3200]{2,1,0:T(2,128)(2,1)}), bf16[32,2,3200]{2,1,0:T(2,128)(2,1)S(1)}, u32[]{:S(2)}, u32[]{:S(2)}) async-start(bf16[32,2,3200]{2,1,0:T(2,128)(2,1)} %reshape.166), calls=%async_computation | async-start | bytes 819200 | tf_op jit(solution)/shard_map/all_to_all | solution.py:81
  23.7 11.2 %all-to-all-done = bf16[32,2,3200]{2,1,0:T(2,128)(2,1)S(1)} async-done(((bf16[32,2,3200]{2,1,0:T(2,128)(2,1)}), bf16[32,2,3200]{2,1,0:T(2,128)(2,1)S(1)}, u32[]{:S(2)}, u32[]{:S(2)}) %all-to-all-start) | async-done | bytes 409632 | tf_op jit(solution)/shard_map/all_to_all | solution.py:81
  37.2 17.8 %all_to_all.44 = bf16[32,2,3200]{2,1,0:T(2,128)(2,1)S(1)} all-to-all(bf16[32,2,3200]{2,1,0:T(2,128)(2,1)S(1)} %reshape.168), channel_id=1, replica_groups=mesh['dp'=32,'head_0'=4,'head_1'=2] {'dp'}, dimensions={0} | all-to-all | bytes 819200 | tf_op jit(solution)/shard_map/all_to_all | solution.py:83
  55.4 2.4 reduce
  59.7 38.8 %all-gather = bf16[32,4,1280]{2,1,0:T(4,128)(2,1)S(1)} all-gather(bf16[1,4,1280]{2,1,0:T(4,128)(2,1)S(1)} %bitcast.96), channel_id=1, replica_groups=mesh['dp'=32,'head_0'=4,'head_1'=2] {'dp'}, dimensions={0}, use_global_device_ids=true | all-gather | bytes 337920 | tf_op jit(solution)/shard_map/all_gather | solution.py:135
  100.3 7.2 %all-to-all-start.3 = ((bf16[128,8,160]{0,2,1:T(8,128)(2,1)}), bf16[128,8,160]{0,2,1:T(8,128)(2,1)S(1)}, u32[]{:S(2)}, u32[]{:S(2)}) async-start(bf16[128,8,160]{0,2,1:T(8,128)(2,1)} %copy.63), calls=%async_computation.3 | async-start | bytes 655360 | tf_op jit(solution)/shard_map/all_to_all | solution.py:139
  107.5 64.6 %all_gather.16 = bf16[1280,3,128]{2,0,1:T(8,128)(2,1)S(1)} all-gather(bf16[40,3,128]{2,0,1:T(8,128)(2,1)S(1)} %copy-done.8), channel_id=1, replica_groups=mesh['dp'=32,'head_0'=4,'head_1'=2] {'dp'}, dimensions={0}, use_global_device_ids=true | all-gather | bytes 1013760 | tf_op jit(solution)/shard_map/all_gather | solution.py:122
  172.9 2.6 convert_reduce_fusion.1
  180.9 2.4 fusion.50
  183.4 8.4 %while.10 = (s32[]{:T(128)}, bf16[2,1280,64]{1,2,0:T(8,128)(2,1)}, bf16[2,1280,64]{2,1,0:T(8,128)(2,1)S(1)}, bf16[2,1280,64]{2,1,0:T(8,128)(2,1)S(1)}, bf16[2,1280,64]{2,1,0:T(8,128)(2,1)}, /*index=5*/s32[]{:T(128)}) while((s32[]{:T(128)}, bf16[2,1280,64]{1,2,0:T(8,128)(2,1)}, bf16[2,1280,64]{2,1,0:T(8,128)(2,1)S(1)}, ...), condition=%wide.region_7.8_spmd, body=%wide.region_4.7_spmd.sunk | while | flops 429340160 | bytes 24773784 | solution.py:61
  191.8 2.6 broadcast_in_dim.36
  194.4 8.3 %all-to-all-start.2 = ((bf16[8,1280,128]{1,2,0:T(8,128)(2,1)}), bf16[8,1280,128]{1,2,0:T(8,128)(2,1)S(1)}, u32[]{:S(2)}, u32[]{:S(2)}) async-start(bf16[8,1280,128]{1,2,0:T(8,128)(2,1)} %broadcast_in_dim.36), calls=%async_computation.2 | async-start | bytes 5242880 | tf_op jit(solution)/shard_map/all_to_all | solution.py:21
  204.2 61.5 %all-to-all-done.2 = bf16[8,1280,128]{1,2,0:T(8,128)(2,1)S(1)} async-done(((bf16[8,1280,128]{1,2,0:T(8,128)(2,1)}), bf16[8,1280,128]{1,2,0:T(8,128)(2,1)S(1)}, u32[]{:S(2)}, u32[]{:S(2)}) %all-to-all-start.2) | async-done | bytes 2621472 | tf_op jit(solution)/shard_map/all_to_all | solution.py:21
  269.4 12.6 %all-to-all-start.4 = ((bf16[32,40,640]{2,1,0:T(8,128)(2,1)}), bf16[32,40,640]{2,1,0:T(8,128)(2,1)}, u32[]{:S(2)}, u32[]{:S(2)}) async-start(bf16[32,40,640]{2,1,0:T(8,128)(2,1)} %broadcast_in_dim.37), calls=%async_computation.4 | async-start | bytes 3276800 | tf_op jit(solution)/shard_map/all_to_all | solution.py:21
  282.1 31.7 %all-gather.10.cloned.1.call-done = bf16[32,20,1280]{2,1,0:T(8,128)(2,1)} async-done(((bf16[1,20,1280]{2,1,0:T(8,128)(2,1)}), bf16[32,20,1280]{2,1,0:T(8,128)(2,1)}) %all-gather.10.cloned.1.call-update) | async-done | bytes 1638416 | tf_op jit(solution)/shard_map/all_gather | solution.py:151
  313.8 4.1 reshape.150
  317.9 93.8 %all-gather.8.cloned.1.call-done = bf16[1280,1280]{0,1:T(8,128)(2,1)} async-done(((bf16[1280,160]{0,1:T(8,128)(2,1)}), bf16[1280,1280]{0,1:T(8,128)(2,1)}) %all-gather.8.cloned.1.call-update) | async-done | bytes 3276816 | tf_op jit(solution)/shard_map/all_gather | solution.py:45
  411.8 2.6 convert_reduce_fusion
  415.6 15.6 %convolution_convert_fusion = bf16[1280,1280]{0,1:T(8,128)(2,1)} fusion(bf16[640,1280]{1,0:T(8,128)(2,1)} %reshape.150, bf16[1280,640]{1,0:T(8,128)(2,1)} %bitcast.24, bf16[1280,1280]{0,1:T(8,128)(2,1)S(1)} %copy-done.1, f32[1280]{0:T(1024)S(1)} %copy-done.15, f32[1280]{0:T(1024)S(1)} %copy-done.16, f32[1280]{0:T(1024)S(1)} %add_rsqrt_fusion, ...), kind=kOutput, calls=%fused_computation.25 | convolution fusion | flops 4259840000 | bytes 9853440 | tf_op jit(solution)/shard_map/dot_general | solution.py:89
  431.2 4.0 copy.71
  435.3 37.3 %reduce-scatter.3.cloned.1.call-done = bf16[2560,160]{0,1:T(8,128)(2,1)} async-done(((bf16[10240,160]{0,1:T(8,128)(2,1)}), bf16[2560,160]{0,1:T(8,128)(2,1)}) %reduce-scatter.3.cloned.1.call-update) | async-done | bytes 819216 | tf_op jit(solution)/shard_map/reduce_scatter | solution.py:31
  472.7 35.9 %reduce-scatter.5.cloned.1.call-done = bf16[1280,160]{0,1:T(8,128)(2,1)} async-done(((bf16[2560,160]{0,1:T(8,128)(2,1)}), bf16[1280,160]{0,1:T(8,128)(2,1)}) %reduce-scatter.5.cloned.1.call-update) | async-done | bytes 409616 | tf_op jit(solution)/shard_map/reduce_scatter | solution.py:31
  (104 shorter events, 32.2 us)
Async XLA Ops:
  7.4 16.0 %copy-start.18 = (s32[32]{0:T(128)S(1)}, s32[32]{0:T(128)}, u32[]{:S(2)}) copy-start(s32[32]{0:T(128)} %param.29) | copy-start | bytes 388
  14.3 20.7 %all-to-all-start = ((bf16[32,2,3200]{2,1,0:T(2,128)(2,1)}), bf16[32,2,3200]{2,1,0:T(2,128)(2,1)S(1)}, u32[]{:S(2)}, u32[]{:S(2)}) async-start(bf16[32,2,3200]{2,1,0:T(2,128)(2,1)} %reshape.166), calls=%async_computation | async-start | bytes 819200 | tf_op jit(solution)/shard_map/all_to_all | solution.py:81
  23.3 149.6 %all-gather.6.cloned.1.call-start = ((), (), s32[]{:S(2)}) async-start(), calls=%async_computation.7 | async-start | bytes 3686400 | tf_op jit(solution)/shard_map/all_gather | solution.py:45
  37.1 22.6 %copy-start.9 = (bf16[4,1280]{1,0:T(4,128)(2,1)S(1)}, bf16[4,1280]{1,0:T(4,128)(2,1)}, u32[]{:S(2)}) copy-start(bf16[4,1280]{1,0:T(4,128)(2,1)} %param.21) | copy-start | bytes 30724
  55.4 52.1 %copy-start.8 = (bf16[40,3,128]{2,0,1:T(8,128)(2,1)S(1)}, bf16[40,3,128]{2,0,1:T(8,128)(2,1)}, u32[]{:S(2)}) copy-start(bf16[40,3,128]{2,0,1:T(8,128)(2,1)} %param.19) | copy-start | bytes 92164
  59.7 113.0 %copy-start.10 = (f32[2,128]{1,0:T(2,128)S(1)}, f32[2,128]{1,0:T(2,128)}, u32[]{:S(2)}) copy-start(f32[2,128]{1,0:T(2,128)} %param.20) | copy-start | bytes 3076
  100.3 91.5 %all-to-all-start.3 = ((bf16[128,8,160]{0,2,1:T(8,128)(2,1)}), bf16[128,8,160]{0,2,1:T(8,128)(2,1)S(1)}, u32[]{:S(2)}, u32[]{:S(2)}) async-start(bf16[128,8,160]{0,2,1:T(8,128)(2,1)} %copy.63), calls=%async_computation.3 | async-start | bytes 655360 | tf_op jit(solution)/shard_map/all_to_all | solution.py:139
  172.9 3.9 copy-start.13
  172.9 3.9 copy-start.14
  172.9 2.9 copy-start
  194.4 71.2 %copy-start.2 = (bf16[1280,160]{0,1:T(8,128)(2,1)S(1)}, bf16[1280,160]{0,1:T(8,128)(2,1)}, u32[]{:S(2)}) copy-start(bf16[1280,160]{0,1:T(8,128)(2,1)} %copy.56) | copy-start | bytes 1228804
  194.4 71.2 %copy-start.12 = (f32[160]{0:T(256)S(1)}, f32[160]{0:T(256)}, u32[]{:S(2)}) copy-start(f32[160]{0:T(256)} %param.22) | copy-start | bytes 1924
  194.4 71.2 %all-to-all-start.2 = ((bf16[8,1280,128]{1,2,0:T(8,128)(2,1)}), bf16[8,1280,128]{1,2,0:T(8,128)(2,1)S(1)}, u32[]{:S(2)}, u32[]{:S(2)}) async-start(bf16[8,1280,128]{1,2,0:T(8,128)(2,1)} %broadcast_in_dim.36), calls=%async_computation.2 | async-start | bytes 5242880 | tf_op jit(solution)/shard_map/all_to_all | solution.py:21
  202.7 65.3 %copy-start.7 = (bf16[40,640]{1,0:T(8,128)(2,1)S(1)}, bf16[40,640]{1,0:T(8,128)(2,1)}, u32[]{:S(2)}) copy-start(bf16[40,640]{1,0:T(8,128)(2,1)} %param.25) | copy-start | bytes 153604
  202.7 111.1 %all-gather.10.cloned.1.call-start = ((), (), s32[]{:S(2)}) async-start(), calls=%async_computation.11 | async-start | bytes 2027520 | tf_op jit(solution)/shard_map/all_gather | solution.py:151
  203.3 208.5 %all-gather.8.cloned.1.call-start = ((), (), s32[]{:S(2)}) async-start(), calls=%async_computation.8 | async-start | bytes 3686400 | tf_op jit(solution)/shard_map/all_gather | solution.py:45
  269.4 146.2 %all-to-all-start.4 = ((bf16[32,40,640]{2,1,0:T(8,128)(2,1)}), bf16[32,40,640]{2,1,0:T(8,128)(2,1)}, u32[]{:S(2)}, u32[]{:S(2)}) async-start(bf16[32,40,640]{2,1,0:T(8,128)(2,1)} %broadcast_in_dim.37), calls=%async_computation.4 | async-start | bytes 3276800 | tf_op jit(solution)/shard_map/all_to_all | solution.py:21
  282.0 190.6 %reduce-scatter.3.cloned.1.call-start = ((), (), s32[]{:S(2)}) async-start(), calls=%async_computation.9 | async-start | bytes 4096000 | tf_op jit(solution)/shard_map/reduce_scatter | solution.py:31
  317.9 97.7 %copy-start.15 = (f32[1280]{0:T(1024)S(1)}, f32[1280]{0:T(1024)}, u32[]{:S(2)}) copy-start(f32[1280]{0:T(1024)} %param.24) | copy-start | bytes 15364
  317.9 97.7 %copy-start.16 = (f32[1280]{0:T(1024)S(1)}, f32[1280]{0:T(1024)}, u32[]{:S(2)}) copy-start(f32[1280]{0:T(1024)} %param.23) | copy-start | bytes 15364
  317.9 97.7 %copy-start.17 = (f32[640]{0:T(1024)S(1)}, f32[640]{0:T(1024)}, u32[]{:S(2)}) copy-start(f32[640]{0:T(1024)} %param.26) | copy-start | bytes 7684
  435.2 73.3 %copy-start.3 = (bf16[1280,160]{0,1:T(8,128)(2,1)S(1)}, bf16[1280,160]{0,1:T(8,128)(2,1)}, u32[]{:S(2)}) copy-start(bf16[1280,160]{0,1:T(8,128)(2,1)} %fusion.46) | copy-start | bytes 1228804
  435.2 73.3 %copy-start.11 = (f32[160]{0:T(256)S(1)}, f32[160]{0:T(256)}, u32[]{:S(2)}) copy-start(f32[160]{0:T(256)} %param.28) | copy-start | bytes 1924
  435.3 73.3 %reduce-scatter.5.cloned.1.call-start = ((), (), s32[]{:S(2)}) async-start(), calls=%async_computation.10 | async-start | bytes 1228800 | tf_op jit(solution)/shard_map/reduce_scatter | solution.py:31
  (7 other events, 8.9 us)
Sparse Core Ops, SparseCore 0:
  59.8 99.7 all-gather.5
  435.4 37.2 reduce-scatter.2
Sparse Core Ops, SparseCore 1:
  205.1 108.7 all-gather.9
  316.3 95.4 all-gather.7
  472.8 35.7 reduce-scatter.4
where the time goes:
time: 528 us; the launch traced here: 519 us
  waiting for transfers between devices  272 us (52%)
  blocking collectives  121 us (23%)
  starting transfers between devices  37.3 us (7%)
  local copies, waits for them, and re-layouts  29.5 us (6%)
  matrix products  24.3 us (5%)
  other arithmetic  19.4 us (4%)
  between operations  15.5 us (3%)
    all_gather x2, waiting for transfers between devices, normalize(): whole_rows = lax.all_gather(residual_in, HEAD, axis=1, tiled=True)  93.8 us
    reduce_scatter x2, waiting for transfers between devices, own_rows(): total = lax.psum_scatter(total, axis, scatter_dimension=0, tiled=True)  73.2 us
    all_gather x1, blocking collectives, on_device(): weight_piece = lax.all_gather(qkv_weight, 'dp', axis=0, tiled=True)  64.6 us
    all_to_all x2, waiting for transfers between devices, sent_to_all(): return lax.all_to_all(copies, axis, split_axis=0, concat_axis=0, tiled=True)  61.5 us
    all_gather x1, blocking collectives, on_device(): output_rows = lax.all_gather(out_weight, 'dp', axis=0, tiled=True)  38.8 us
    all_gather x1, waiting for transfers between devices, on_device(): down_rows = lax.all_gather(fc2_weight, 'dp', axis=0, tiled=True)  31.7 us
    all_to_all x2, starting transfers between devices, sent_to_all(): return lax.all_to_all(copies, axis, split_axis=0, concat_axis=0, tiled=True)  20.9 us
    all_to_all x1, blocking collectives, regroup(): lax.all_to_all(picked, 'dp', split_axis=0, concat_axis=0, tiled=True)  17.8 us
  transfers between devices with their start and end apart: 9, of which 6 were waited for; matrix products, arithmetic and copies ran while one was open for 6% of the time, Pallas kernels for 0%

commit v1 on v0

--- a/solution.py
+++ b/solution.py
@@ -8,6 +8,13 @@
 HEAD = ("head_0", "head_1")
 HEAD_DP = ("head_0", "head_1", "dp")
 epsilon = 1e-05
+
+
+def swapped_in(block, name, d):
+    devices = lax.axis_size(name)
+    blocks = jnp.stack([block for _ in range(devices)])
+    blocks = lax.all_to_all(blocks, name, split_axis=0, concat_axis=0)
+    return jnp.concatenate(blocks, axis=d)
 
 
 def laid_out(blocks, dim):
@@ -132,7 +139,7 @@
     key_rows = projected[:, 1].astype(jnp.bfloat16).reshape(frame_count, -1, HDIM)
     value_rows = (projected[:, 2] + qv_bias[1]).astype(jnp.bfloat16).reshape(frame_count, -1, HDIM)
     context = attend(queries, key_rows, value_rows)
-    output_rows = lax.all_gather(out_weight, "dp", axis=0, tiled=True)
+    output_rows = swapped_in(out_weight, "dp", 0)
     carried = residual_in.astype(jnp.float32) + out_bias
     whole_context = gather_directly(context, HEAD, 1)
     split_rows = output_rows.reshape(output_rows.shape[0], head_count, local_width)

time: 528 us -> 512 us (0.970)
  blocking collectives: 121 us -> 67.6 us
  starting transfers between devices: 37.3 us -> 79.9 us
  waiting for transfers between devices: 272 us -> 266 us
    all_gather x1 -> x0, blocking collectives: 38.8 us -> none  [on_device(): output_rows = lax.all_gather(out_weight, 'dp', axis=0, tiled=True)]
    all_gather x2, waiting for transfers between devices: 93.8 us -> 124 us  [normalize(): whole_rows = lax.all_gather(residual_in, HEAD, axis=1, tiled=True)]
    all_to_all x2, waiting for transfers between devices: 61.5 us -> 32.6 us  [sent_to_all(): return lax.all_to_all(copies, axis, split_axis=0, concat_axis=0, tiled=True)]
    all_to_all x2, starting transfers between devices: 20.9 us -> 46.1 us  [sent_to_all(): return lax.all_to_all(copies, axis, split_axis=0, concat_axis=0, tiled=True)]
    all_gather x1, blocking collectives: 64.6 us -> 49.8 us  [on_device(): weight_piece = lax.all_gather(qkv_weight, 'dp', axis=0, tiled=True)]
    all_to_all x1, starting transfers between devices: 7.22 us -> 18.1 us  [on_device(): lax.all_to_all(split_rows, HEAD, split_axis=1, concat_axis=0, tiled=True)]
    all_gather x1, waiting for transfers between devices: 31.7 us -> 23.9 us  [on_device(): down_rows = lax.all_gather(fc2_weight, 'dp', axis=0, tiled=True)]
    all_to_all x0 -> x1, starting transfers between devices: none -> 6.39 us  [swapped_in(): blocks = lax.all_to_all(blocks, name, split_axis=0, concat_axis=0)]
  transfers between devices with their start and end apart: 9 -> 10, of which waited for: 6 -> 7; matrix products, arithmetic and copies ran while one was open for 6% -> 6% of each run, Pallas kernels for 0% -> 0%
where the time goes in v1:
time: 512 us; the launch traced here: 503 us
  waiting for transfers between devices  266 us (52%)
  starting transfers between devices  79.9 us (16%)
  blocking collectives  67.6 us (13%)
  local copies, waits for them, and re-layouts  29.9 us (6%)
  matrix products  24.4 us (5%)
  other arithmetic  19.3 us (4%)
  between operations  15.7 us (3%)
    all_gather x2, waiting for transfers between devices, normalize(): whole_rows = lax.all_gather(residual_in, HEAD, axis=1, tiled=True)  124 us
    reduce_scatter x2, waiting for transfers between devices, own_rows(): total = lax.psum_scatter(total, axis, scatter_dimension=0, tiled=True)  73.2 us
    all_gather x1, blocking collectives, on_device(): weight_piece = lax.all_gather(qkv_weight, 'dp', axis=0, tiled=True)  49.8 us
    all_to_all x2, starting transfers between devices, sent_to_all(): return lax.all_to_all(copies, axis, split_axis=0, concat_axis=0, tiled=True)  46.1 us
    all_to_all x2, waiting for transfers between devices, sent_to_all(): return lax.all_to_all(copies, axis, split_axis=0, concat_axis=0, tiled=True)  32.6 us
    all_gather x1, waiting for transfers between devices, on_device(): down_rows = lax.all_gather(fc2_weight, 'dp', axis=0, tiled=True)  23.9 us
    all_to_all x1, starting transfers between devices, on_device(): lax.all_to_all(split_rows, HEAD, split_axis=1, concat_axis=0, tiled=True)  18.1 us
    all_to_all x1, blocking collectives, regroup(): lax.all_to_all(picked, 'dp', split_axis=0, concat_axis=0, tiled=True)  17.8 us
  transfers between devices with their start and end apart: 10, of which 7 were waited for; matrix products, arithmetic and copies ran while one was open for 6% of the time, Pallas kernels for 0%

profile of v1, /device:TPU:2, one launch (start us, length us, event | category | flops | bytes accessed | tf_op | source)
XLA Modules:
  0.0 502.7 jit_solution(14783118371410706284)
XLA Ops:
  10.3 3.0 reduce.9
  14.2 9.1 %all-to-all-start = ((bf16[32,2,3200]{2,1,0:T(2,128)(2,1)}), bf16[32,2,3200]{2,1,0:T(2,128)(2,1)S(1)}, u32[]{:S(2)}, u32[]{:S(2)}) async-start(bf16[32,2,3200]{2,1,0:T(2,128)(2,1)} %reshape.161), calls=%async_computation | async-start | bytes 819200 | tf_op jit(solution)/shard_map/all_to_all | solution.py:88
  23.6 11.2 %all-to-all-done = bf16[32,2,3200]{2,1,0:T(2,128)(2,1)S(1)} async-done(((bf16[32,2,3200]{2,1,0:T(2,128)(2,1)}), bf16[32,2,3200]{2,1,0:T(2,128)(2,1)S(1)}, u32[]{:S(2)}, u32[]{:S(2)}) %all-to-all-start) | async-done | bytes 409632 | tf_op jit(solution)/shard_map/all_to_all | solution.py:88
  37.2 17.8 %all_to_all.49 = bf16[32,2,3200]{2,1,0:T(2,128)(2,1)S(1)} all-to-all(bf16[32,2,3200]{2,1,0:T(2,128)(2,1)S(1)} %reshape.163), channel_id=1, replica_groups=mesh['dp'=32,'head_0'=4,'head_1'=2] {'dp'}, dimensions={0} | all-to-all | bytes 819200 | tf_op jit(solution)/shard_map/all_to_all | solution.py:90
  55.3 2.4 reduce
  60.4 6.4 %all-to-all-start.3 = ((bf16[32,4,1280]{2,1,0:T(4,128)(2,1)}), bf16[32,4,1280]{2,1,0:T(4,128)(2,1)S(1)}, u32[]{:S(2)}, u32[]{:S(2)}) async-start(bf16[32,4,1280]{2,1,0:T(4,128)(2,1)} %stack.2), calls=%async_computation.3 | async-start | bytes 655360 | tf_op jit(solution)/shard_map/all_to_all | solution.py:16
  66.9 49.8 %all_gather.13 = bf16[1280,3,128]{2,0,1:T(8,128)(2,1)S(1)} all-gather(bf16[40,3,128]{2,0,1:T(8,128)(2,1)S(1)} %copy-done.8), channel_id=1, replica_groups=mesh['dp'=32,'head_0'=4,'head_1'=2] {'dp'}, dimensions={0}, use_global_device_ids=true | all-gather | bytes 1013760 | tf_op jit(solution)/shard_map/all_gather | solution.py:129
  119.2 18.1 %all-to-all-start.4 = ((bf16[128,8,160]{0,2,1:T(8,128)(2,1)}), bf16[128,8,160]{0,2,1:T(8,128)(2,1)S(1)}, u32[]{:S(2)}, u32[]{:S(2)}) async-start(bf16[128,8,160]{0,2,1:T(8,128)(2,1)} %copy.63), calls=%async_computation.4 | async-start | bytes 655360 | tf_op jit(solution)/shard_map/all_to_all | solution.py:146
  137.3 20.6 %all-gather.5.cloned.1.call-done = bf16[1280,1280]{0,1:T(8,128)(2,1)} async-done(((bf16[1280,160]{0,1:T(8,128)(2,1)}), bf16[1280,1280]{0,1:T(8,128)(2,1)}) %all-gather.5.cloned.1.call-update) | async-done | bytes 3276816 | tf_op jit(solution)/shard_map/all_gather | solution.py:52
  157.9 2.6 convert_reduce_fusion.1
  165.9 2.4 fusion.50
  168.3 8.4 %while.10 = (s32[]{:T(128)}, bf16[2,1280,64]{1,2,0:T(8,128)(2,1)}, bf16[2,1280,64]{2,1,0:T(8,128)(2,1)S(1)}, bf16[2,1280,64]{2,1,0:T(8,128)(2,1)S(1)}, bf16[2,1280,64]{2,1,0:T(8,128)(2,1)}, /*index=5*/s32[]{:T(128)}) while((s32[]{:T(128)}, bf16[2,1280,64]{1,2,0:T(8,128)(2,1)}, bf16[2,1280,64]{2,1,0:T(8,128)(2,1)S(1)}, ...), condition=%wide.region_7.8_spmd, body=%wide.region_4.7_spmd.sunk | while | flops 429340160 | bytes 24773784 | solution.py:68
  176.7 2.6 broadcast_in_dim.36
  179.4 3.8 all-to-all-start.2
  184.6 32.6 %all-to-all-done.2 = bf16[8,1280,128]{1,2,0:T(8,128)(2,1)S(1)} async-done(((bf16[8,1280,128]{1,2,0:T(8,128)(2,1)}), bf16[8,1280,128]{1,2,0:T(8,128)(2,1)S(1)}, u32[]{:S(2)}, u32[]{:S(2)}) %all-to-all-start.2) | async-done | bytes 2621472 | tf_op jit(solution)/shard_map/all_to_all | solution.py:28
  221.0 42.4 %all-to-all-start.5 = ((bf16[32,40,640]{2,1,0:T(8,128)(2,1)}), bf16[32,40,640]{2,1,0:T(8,128)(2,1)}, u32[]{:S(2)}, u32[]{:S(2)}) async-start(bf16[32,40,640]{2,1,0:T(8,128)(2,1)} %broadcast_in_dim.37), calls=%async_computation.5 | async-start | bytes 3276800 | tf_op jit(solution)/shard_map/all_to_all | solution.py:28
  263.4 23.9 %all-gather.9.cloned.1.call-done = bf16[32,20,1280]{2,1,0:T(8,128)(2,1)} async-done(((bf16[1,20,1280]{2,1,0:T(8,128)(2,1)}), bf16[32,20,1280]{2,1,0:T(8,128)(2,1)}) %all-gather.9.cloned.1.call-update) | async-done | bytes 1638416 | tf_op jit(solution)/shard_map/all_gather | solution.py:158
  287.3 3.8 reshape.146
  291.2 103.8 %all-gather.7.cloned.1.call-done = bf16[1280,1280]{0,1:T(8,128)(2,1)} async-done(((bf16[1280,160]{0,1:T(8,128)(2,1)}), bf16[1280,1280]{0,1:T(8,128)(2,1)}) %all-gather.7.cloned.1.call-update) | async-done | bytes 3276816 | tf_op jit(solution)/shard_map/all_gather | solution.py:52
  394.9 2.6 convert_reduce_fusion
  398.8 15.6 %convolution_convert_fusion = bf16[1280,1280]{0,1:T(8,128)(2,1)} fusion(bf16[640,1280]{1,0:T(8,128)(2,1)} %reshape.146, bf16[1280,640]{1,0:T(8,128)(2,1)} %bitcast.23, bf16[1280,1280]{0,1:T(8,128)(2,1)S(1)} %copy-done.1, f32[1280]{0:T(1024)S(1)} %copy-done.15, f32[1280]{0:T(1024)S(1)} %copy-done.16, f32[1280]{0:T(1024)S(1)} %add_rsqrt_fusion, ...), kind=kOutput, calls=%fused_computation.25 | convolution fusion | flops 4259840000 | bytes 9853440 | tf_op jit(solution)/shard_map/dot_general | solution.py:96
  414.4 4.0 copy.71
  418.5 37.3 %reduce-scatter.3.cloned.1.call-done = bf16[2560,160]{0,1:T(8,128)(2,1)} async-done(((bf16[10240,160]{0,1:T(8,128)(2,1)}), bf16[2560,160]{0,1:T(8,128)(2,1)}) %reduce-scatter.3.cloned.1.call-update) | async-done | bytes 819216 | tf_op jit(solution)/shard_map/reduce_scatter | solution.py:38
  455.9 35.9 %reduce-scatter.5.cloned.1.call-done = bf16[1280,160]{0,1:T(8,128)(2,1)} async-done(((bf16[2560,160]{0,1:T(8,128)(2,1)}), bf16[1280,160]{0,1:T(8,128)(2,1)}) %reduce-scatter.5.cloned.1.call-update) | async-done | bytes 409616 | tf_op jit(solution)/shard_map/reduce_scatter | solution.py:38
  (106 shorter events, 35.2 us)
Async XLA Ops:
  7.4 15.9 %copy-start.18 = (s32[32]{0:T(128)S(1)}, s32[32]{0:T(128)}, u32[]{:S(2)}) copy-start(s32[32]{0:T(128)} %param.29) | copy-start | bytes 388
  14.2 20.7 %all-to-all-start = ((bf16[32,2,3200]{2,1,0:T(2,128)(2,1)}), bf16[32,2,3200]{2,1,0:T(2,128)(2,1)S(1)}, u32[]{:S(2)}, u32[]{:S(2)}) async-start(bf16[32,2,3200]{2,1,0:T(2,128)(2,1)} %reshape.161), calls=%async_computation | async-start | bytes 819200 | tf_op jit(solution)/shard_map/all_to_all | solution.py:88
  23.2 134.7 %all-gather.5.cloned.1.call-start = ((), (), s32[]{:S(2)}) async-start(), calls=%async_computation.8 | async-start | bytes 3686400 | tf_op jit(solution)/shard_map/all_gather | solution.py:52
  37.0 22.6 %copy-start.9 = (bf16[4,1280]{1,0:T(4,128)(2,1)S(1)}, bf16[4,1280]{1,0:T(4,128)(2,1)}, u32[]{:S(2)}) copy-start(bf16[4,1280]{1,0:T(4,128)(2,1)} %param.21) | copy-start | bytes 30724
  37.2 29.7 %copy-start.8 = (bf16[40,3,128]{2,0,1:T(8,128)(2,1)S(1)}, bf16[40,3,128]{2,0,1:T(8,128)(2,1)}, u32[]{:S(2)}) copy-start(bf16[40,3,128]{2,0,1:T(8,128)(2,1)} %param.19) | copy-start | bytes 92164
  57.8 59.5 %copy-start.10 = (f32[2,128]{1,0:T(2,128)S(1)}, f32[2,128]{1,0:T(2,128)}, u32[]{:S(2)}) copy-start(f32[2,128]{1,0:T(2,128)} %param.20) | copy-start | bytes 3076
  60.4 57.0 %all-to-all-start.3 = ((bf16[32,4,1280]{2,1,0:T(4,128)(2,1)}), bf16[32,4,1280]{2,1,0:T(4,128)(2,1)S(1)}, u32[]{:S(2)}, u32[]{:S(2)}) async-start(bf16[32,4,1280]{2,1,0:T(4,128)(2,1)} %stack.2), calls=%async_computation.3 | async-start | bytes 655360 | tf_op jit(solution)/shard_map/all_to_all | solution.py:16
  119.2 57.5 %all-to-all-start.4 = ((bf16[128,8,160]{0,2,1:T(8,128)(2,1)}), bf16[128,8,160]{0,2,1:T(8,128)(2,1)S(1)}, u32[]{:S(2)}, u32[]{:S(2)}) async-start(bf16[128,8,160]{0,2,1:T(8,128)(2,1)} %copy.63), calls=%async_computation.4 | async-start | bytes 655360 | tf_op jit(solution)/shard_map/all_to_all | solution.py:146
  137.3 24.4 %copy-start.13 = (f32[1280]{0:T(1024)S(1)}, f32[1280]{0:T(1024)}, u32[]{:S(2)}) copy-start(f32[1280]{0:T(1024)} %param.18) | copy-start | bytes 15364
  137.3 24.4 %copy-start.14 = (f32[1280]{0:T(1024)S(1)}, f32[1280]{0:T(1024)}, u32[]{:S(2)}) copy-start(f32[1280]{0:T(1024)} %param.17) | copy-start | bytes 15364
  179.3 37.9 %copy-start.2 = (bf16[1280,160]{0,1:T(8,128)(2,1)S(1)}, bf16[1280,160]{0,1:T(8,128)(2,1)}, u32[]{:S(2)}) copy-start(bf16[1280,160]{0,1:T(8,128)(2,1)} %copy.56) | copy-start | bytes 1228804
  179.4 37.9 %copy-start.12 = (f32[160]{0:T(256)S(1)}, f32[160]{0:T(256)}, u32[]{:S(2)}) copy-start(f32[160]{0:T(256)} %param.22) | copy-start | bytes 1924
  179.4 37.9 %all-to-all-start.2 = ((bf16[8,1280,128]{1,2,0:T(8,128)(2,1)}), bf16[8,1280,128]{1,2,0:T(8,128)(2,1)S(1)}, u32[]{:S(2)}, u32[]{:S(2)}) async-start(bf16[8,1280,128]{1,2,0:T(8,128)(2,1)} %broadcast_in_dim.36), calls=%async_computation.2 | async-start | bytes 5242880 | tf_op jit(solution)/shard_map/all_to_all | solution.py:28
  183.1 36.5 %copy-start.7 = (bf16[40,640]{1,0:T(8,128)(2,1)S(1)}, bf16[40,640]{1,0:T(8,128)(2,1)}, u32[]{:S(2)}) copy-start(bf16[40,640]{1,0:T(8,128)(2,1)} %param.25) | copy-start | bytes 153604
  183.1 104.2 %all-gather.9.cloned.1.call-start = ((), (), s32[]{:S(2)}) async-start(), calls=%async_computation.12 | async-start | bytes 2027520 | tf_op jit(solution)/shard_map/all_gather | solution.py:158
  183.7 211.2 %all-gather.7.cloned.1.call-start = ((), (), s32[]{:S(2)}) async-start(), calls=%async_computation.9 | async-start | bytes 3686400 | tf_op jit(solution)/shard_map/all_gather | solution.py:52
  221.0 177.8 %all-to-all-start.5 = ((bf16[32,40,640]{2,1,0:T(8,128)(2,1)}), bf16[32,40,640]{2,1,0:T(8,128)(2,1)}, u32[]{:S(2)}, u32[]{:S(2)}) async-start(bf16[32,40,640]{2,1,0:T(8,128)(2,1)} %broadcast_in_dim.37), calls=%async_computation.5 | async-start | bytes 3276800 | tf_op jit(solution)/shard_map/all_to_all | solution.py:28
  263.3 192.5 %reduce-scatter.3.cloned.1.call-start = ((), (), s32[]{:S(2)}) async-start(), calls=%async_computation.10 | async-start | bytes 4096000 | tf_op jit(solution)/shard_map/reduce_scatter | solution.py:38
  291.1 107.6 %copy-start.15 = (f32[1280]{0:T(1024)S(1)}, f32[1280]{0:T(1024)}, u32[]{:S(2)}) copy-start(f32[1280]{0:T(1024)} %param.24) | copy-start | bytes 15364
  291.1 107.6 %copy-start.16 = (f32[1280]{0:T(1024)S(1)}, f32[1280]{0:T(1024)}, u32[]{:S(2)}) copy-start(f32[1280]{0:T(1024)} %param.23) | copy-start | bytes 15364
  291.1 107.6 %copy-start.17 = (f32[640]{0:T(1024)S(1)}, f32[640]{0:T(1024)}, u32[]{:S(2)}) copy-start(f32[640]{0:T(1024)} %param.26) | copy-start | bytes 7684
  418.4 73.3 %copy-start.3 = (bf16[1280,160]{0,1:T(8,128)(2,1)S(1)}, bf16[1280,160]{0,1:T(8,128)(2,1)}, u32[]{:S(2)}) copy-start(bf16[1280,160]{0,1:T(8,128)(2,1)} %fusion.46) | copy-start | bytes 1228804
  418.4 73.3 %copy-start.11 = (f32[160]{0:T(256)S(1)}, f32[160]{0:T(256)}, u32[]{:S(2)}) copy-start(f32[160]{0:T(256)} %param.28) | copy-start | bytes 1924
  418.5 73.3 %reduce-scatter.5.cloned.1.call-start = ((), (), s32[]{:S(2)}) async-start(), calls=%async_computation.11 | async-start | bytes 1228800 | tf_op jit(solution)/shard_map/reduce_scatter | solution.py:38
  (8 other events, 11.8 us)
Sparse Core Ops, SparseCore 0:
  59.7 98.1 all-gather.4
  418.6 37.2 reduce-scatter.2
Sparse Core Ops, SparseCore 1:
  185.5 101.8 all-gather.8
  289.8 105.0 all-gather.6
  456.0 35.7 reduce-scatter.4
